TPU v7x, 32 devices: a whole 2x2x4 slice. The times are simulated.
32 devices in a mesh: group: 4 (over y, core), member: 8 (over z, x).
Axes of the slice: x: 2, y: 2, z: 4, core: 2. Of those that a mesh axis runs over, the one named last changes fastest.
Arguments:
- off_tiles: bfloat16 [64, 8, 128, 128], P(('group', 'member')), may hold values from -0.1875 to 0.1875
- off_cols: int32 [64, 8], P(('group', 'member')), may hold values from 0 to 17
- member_send: int32 [32, 8, 1], P(('group', 'member')), may hold values from 0 to 1
- group_send: int32 [32, 4], P(('group', 'member')), may hold values from 0 to 1
- diag_tiles: bfloat16 [64, 128, 128], P(('group', 'member')), may hold values from -1 to 9
- smoother: bfloat16 [64, 128, 128], P(('group', 'member')), may hold values from -1 to 1
- agg_map: int32 [64], P(('group', 'member')), may hold values from 0 to 1
- prolong: bfloat16 [64, 128, 128], P(('group', 'member')), may hold values from -0.5 to 0.5
- coarse_inv: bfloat16 [1024, 1024], P(None, 'group'), may hold values from -0.03125 to 0.03125
- krylov_basis: bfloat16 [64, 32, 128], P(('group', 'member')), may hold values from -24 to 24, as said below
Outputs:
- preconditioned: bfloat16 [64, 8, 128], P(('group', 'member'))
- coefficients: float32 [32, 8], replicated
- gram_matrix: float32 [8, 8], replicated
- new_block: float32 [64, 8, 128], P(('group', 'member'))
Inputs may be any that keep to these rules, and one draw needn't show every extreme that they name: `off_cols`: entries below 2 name the device's own row tiles; entry 2 + p + s names slot s of what member p of the same group sends; the last 8 entries name what the groups below and above send. `member_send`: entry [d, p, s] is the local row tile that device d sends to member p of its group in slot s. `group_send`: entry [d, s] is the local row tile that device d sends, in slot s, to the same member of the groups below and above. `krylov_basis`: the 32 basis vectors are orthonormal, up to bfloat16 rounding, under the inner product (1 / 8192) times the sum over all rows.
All inputs are finite; a program needn't handle non-finite values.
Results may differ from a plain program's by a relative error of at most 0.02.
Values may be sent and summed in bfloat16 or wider, within the bound.
No kernel may reach another device: no remote copies, remote signals or barrier semaphores. Data moves between devices by JAX's collectives and lax.ppermute only.
A program may use at most 64 MiB of HBM per device.

v0:
```python
import jax
import jax.numpy as jnp
from jax import lax
from jax.sharding import PartitionSpec as P

TILE = 128
NVEC = 8
GH = 1
CTG = 2


def extended_2(cells, sides, width):
    for axis, dim in sides:
        count = lax.axis_size(axis)
        ends = count - 1
        head = lax.slice_in_dim(cells, 0, width, axis=dim)
        tail = lax.slice_in_dim(cells, cells.shape[dim] - width, cells.shape[dim], axis=dim)
        cells = jnp.concatenate(
            [
                lax.ppermute(tail, axis, [(i, (i + 1) % count) for i in range(ends)]),
                cells,
                lax.ppermute(head, axis, [((i + 1) % count, i) for i in range(ends)]),
            ],
            axis=dim,
        )
    return cells


def extend_tiles(values, member_send, group_send, members):
    outgoing = values[member_send[0].reshape(-1)].reshape(members, GH, NVEC, TILE)
    arrived = lax.all_to_all(outgoing, "member", split_axis=0, concat_axis=0, tiled=True).reshape(
        members * GH, NVEC, TILE
    )
    rim_tiles = values[group_send[0]][None]
    beside = extended_2(rim_tiles, (("group", 0),), 1)
    return jnp.concatenate([values, arrived, beside[0], beside[2]], axis=0)


def operate(values, off_tiles, off_cols, diag_tiles, member_send, group_send, members):
    extended = extend_tiles(values, member_send, group_send, members)
    picked = extended[off_cols]
    far_part = jnp.einsum("tkcj,tkji->tci", picked, off_tiles, preferred_element_type=jnp.float32)
    near_part = jnp.einsum("tcj,tji->tci", values, diag_tiles, preferred_element_type=jnp.float32)
    return near_part + far_part


def tilewise(left_side, tiles):
    return jnp.einsum("tcj,tji->tci", left_side, tiles, preferred_element_type=jnp.float32)


def exact_product(form, first_operand, second_operand):
    return jnp.einsum(form, first_operand, second_operand, precision=lax.Precision.HIGHEST)


def local(
    off_tiles,
    off_cols,
    member_send,
    group_send,
    diag_tiles,
    smoother,
    agg_map,
    prolong,
    coarse_inv,
    krylov_basis,
):
    members = lax.axis_size("member")
    groups = lax.axis_size("group")
    tiles_dev = diag_tiles.shape[0]
    rows_all = tiles_dev * TILE * members * groups
    scale_rows = 1.0 / rows_all

    def apply_operator(values):
        return operate(values, off_tiles, off_cols, diag_tiles, member_send, group_send, members)

    last_block = krylov_basis[:, krylov_basis.shape[1] - NVEC :, :]
    block_wide = last_block.astype(jnp.float32)
    first = tilewise(last_block, smoother).astype(jnp.bfloat16)
    residual_one = (block_wide - apply_operator(first)).astype(jnp.bfloat16)
    pieces = jnp.einsum("tci,tji->tcj", residual_one, prolong, preferred_element_type=jnp.float32)
    selector = (agg_map[:, None] == jnp.arange(CTG, dtype=jnp.int32)[None, :]).astype(jnp.float32)
    coarse_part = exact_product("ta,tcj->acj", selector, pieces)
    spread = jnp.zeros((groups, CTG, NVEC, TILE), jnp.float32)
    spread = lax.dynamic_update_slice(spread, coarse_part[None], (lax.axis_index("group"), 0, 0, 0))
    coarse_all = lax.psum(spread, ("group", "member")).reshape(groups * CTG, NVEC, TILE)
    coarse_round = coarse_all.astype(jnp.bfloat16)
    columns = coarse_inv.reshape(groups * CTG, TILE, CTG * TILE)
    correction = jnp.einsum(
        "acj,ajo->co", coarse_round, columns, preferred_element_type=jnp.float32
    )
    correction = correction.astype(jnp.bfloat16).reshape(NVEC, CTG, TILE)
    chosen = jnp.einsum(
        "ta,cak->tck", selector.astype(jnp.bfloat16), correction, preferred_element_type=jnp.float32
    )
    second = (first.astype(jnp.float32) + tilewise(chosen.astype(jnp.bfloat16), prolong)).astype(
        jnp.bfloat16
    )
    residual_two = (block_wide - apply_operator(second)).astype(jnp.bfloat16)
    preconditioned = (second.astype(jnp.float32) + tilewise(residual_two, smoother)).astype(
        jnp.bfloat16
    )
    applied = apply_operator(preconditioned).astype(jnp.bfloat16)
    coeff_part = (
        jnp.einsum("tpi,tci->pc", krylov_basis, applied, preferred_element_type=jnp.float32)
        * scale_rows
    )
    basis_wide = krylov_basis.astype(jnp.float32)
    self_part = (
        jnp.einsum("tci,tdi->cd", applied, applied, preferred_element_type=jnp.float32) * scale_rows
    )
    basis_part = (
        jnp.einsum("tpi,tqi->pq", krylov_basis, krylov_basis, preferred_element_type=jnp.float32)
        * scale_rows
    )
    coefficients, self_total, basis_total = lax.psum(
        (coeff_part, self_part, basis_part), ("group", "member")
    )
    remainder = applied.astype(jnp.float32) - exact_product("pc,tpi->tci", coefficients, basis_wide)
    cross = exact_product("pc,pd->cd", coefficients, coefficients)
    weighted = exact_product("pq,qd->pd", basis_total, coefficients)
    gram_matrix = self_total - 2.0 * cross + exact_product("pc,pd->cd", coefficients, weighted)
    factor = jnp.linalg.cholesky(gram_matrix)
    inverse = lax.linalg.triangular_solve(
        factor, jnp.eye(NVEC, dtype=jnp.float32), left_side=True, lower=True
    )
    new_block = exact_product("cd,tdi->tci", inverse, remainder)
    return (preconditioned, coefficients, gram_matrix, new_block)


def solution(mesh):
    placed = (
        P(("group", "member"), None, None, None),
        P(("group", "member"), None),
        P(("group", "member"), None, None),
        P(("group", "member"), None),
        P(("group", "member"), None, None),
        P(("group", "member"), None, None),
        P(("group", "member")),
        P(("group", "member"), None, None),
        P(None, "group"),
        P(("group", "member"), None, None),
    )
    return jax.shard_map(
        local,
        mesh=mesh,
        in_specs=placed,
        out_specs=(
            P(("group", "member"), None, None),
            P(),
            P(),
            P(("group", "member"), None, None),
        ),
        check_vma=False,
    )
```

profile of v0, /device:TPU:0, one launch (start us, length us, event | category | flops | bytes accessed | tf_op | source)
XLA Modules:
  0.0 144.9 jit_solution(4221777477460338780)
XLA Ops:
  0.6 0.0 copy-start
  0.6 0.7 fusion.33
  1.4 1.0 convolution_convert_fusion
  2.4 0.6 gather_fusion.1
  2.9 0.0 copy-start.10
  2.9 2.4 %collective-permute-start = (bf16[1,4,8,128]{3,2,1,0:T(8,128)(2,1)S(1)}, bf16[1,4,8,128]{3,2,1,0:T(8,128)(2,1)S(1)}, u32[]{:S(2)}, u32[]{:S(2)}) collective-permute-start(bf16[1,4,8,128]{3,2,1,0:T(8,128)(2,1)S(1)} %bitcast.145), channel_id=1, source_target_pairs={{0,8},{8,16},{16,24},{1,9},{9,17},{17,25},{2,10},{10,18},{18,26},{... | collective-permute-start | bytes 24584 | tf_op jit(solution)/shard_map/ppermute | solution.py:20
  5.3 1.3 collective-permute-start.1
  6.7 1.2 gather_fusion
  7.8 6.8 %all-to-all-start = ((bf16[8,1,8,128]{3,2,1,0:T(8,128)(2,1)}), bf16[8,1,8,128]{3,2,1,0:T(8,128)(2,1)S(1)}, u32[]{:S(2)}, u32[]{:S(2)}) async-start(bf16[8,1,8,128]{3,2,1,0:T(8,128)(2,1)} %bitcast.5), calls=%async_computation | async-start | bytes 32768 | tf_op jit(solution)/shard_map/all_to_all | solution.py:31
  14.6 0.1 reshape.126
  14.7 0.0 collective-permute-done
  14.7 0.0 collective-permute-done.1
  14.7 6.5 %all-to-all-done = bf16[8,1,8,128]{3,2,1,0:T(8,128)(2,1)S(1)} async-done(((bf16[8,1,8,128]{3,2,1,0:T(8,128)(2,1)}), bf16[8,1,8,128]{3,2,1,0:T(8,128)(2,1)S(1)}, u32[]{:S(2)}, u32[]{:S(2)}) %all-to-all-start) | async-done | bytes 16416 | tf_op jit(solution)/shard_map/all_to_all | solution.py:31
  21.2 0.6 gather_fusion.2
  21.8 0.0 copy-start.3
  21.8 0.0 copy-start.6
  21.8 1.3 convolution_bitcast_fusion.7
  23.1 0.0 copy-start.11
  23.1 0.2 fusion.11
  23.3 0.4 copy-done.11
  23.7 0.1 fusion.3
  23.9 41.0 %psum.28 = bf16[4,2,8,128]{3,1,2,0:T(2,128)(2,1)S(1)} all-reduce(f32[4,2,8,128]{3,1,2,0:T(2,128)S(1)} %fusion.3), channel_id=1, replica_groups=mesh['group'=4,'member'=8] {'group','member'}, use_global_device_ids=true, to_apply=%region_0.0 | all-reduce | flops 8192 | bytes 49152 | tf_op jit(solution)/shard_map/psum | solution.py:85
  64.9 0.2 fusion.16
  65.1 0.2 fusion.24
  65.3 0.1 fusion.7
  65.4 1.2 gather_fusion.3
  66.6 4.5 %all-to-all-start.1 = ((bf16[8,1,8,128]{3,2,1,0:T(8,128)(2,1)}), bf16[8,1,8,128]{3,2,1,0:T(8,128)(2,1)S(1)}, u32[]{:S(2)}, u32[]{:S(2)}) async-start(bf16[8,1,8,128]{3,2,1,0:T(8,128)(2,1)} %bitcast.21), calls=%async_computation.1 | async-start | bytes 32768 | tf_op jit(solution)/shard_map/all_to_all | solution.py:31
  71.1 0.6 gather_fusion.4
  71.6 1.3 collective-permute-start.2
  72.9 1.3 collective-permute-start.3
  74.2 0.0 collective-permute-done.2
  74.3 3.6 %collective-permute-done.3 = bf16[1,4,8,128]{3,2,1,0:T(8,128)(2,1)S(1)} collective-permute-done((bf16[1,4,8,128]{3,2,1,0:T(8,128)(2,1)S(1)}, bf16[1,4,8,128]{3,2,1,0:T(8,128)(2,1)S(1)}, u32[]{:S(2)}, u32[]{:S(2)}) %collective-permute-start.3) | collective-permute-done | bytes 8224 | tf_op jit(solution)/shard_map/ppermute | solution.py:22
  77.8 0.0 all-to-all-done.1
  77.8 0.6 gather_fusion.5
  78.4 0.0 copy-start.5
  78.4 0.2 convolution_bitcast_fusion.5
  78.6 0.6 copy-done.5
  79.3 0.2 fusion.9
  79.5 1.2 gather_fusion.6
  80.7 0.6 gather_fusion.7
  81.2 4.3 %collective-permute-start.4 = (bf16[1,4,8,128]{3,2,1,0:T(8,128)(2,1)S(1)}, bf16[1,4,8,128]{3,2,1,0:T(8,128)(2,1)S(1)}, u32[]{:S(2)}, u32[]{:S(2)}) collective-permute-start(bf16[1,4,8,128]{3,2,1,0:T(8,128)(2,1)S(1)} %bitcast.147), channel_id=1, source_target_pairs={{0,8},{8,16},{16,24},{1,9},{9,17},{17,25},{2,10},{10,18},{18,26},{... | collective-permute-start | bytes 24584 | tf_op jit(solution)/shard_map/ppermute | solution.py:20
  85.5 1.3 collective-permute-start.5
  86.8 6.0 %all-to-all-start.2 = ((bf16[8,1,8,128]{3,2,1,0:T(8,128)(2,1)}), bf16[8,1,8,128]{3,2,1,0:T(8,128)(2,1)S(1)}, u32[]{:S(2)}, u32[]{:S(2)}) async-start(bf16[8,1,8,128]{3,2,1,0:T(8,128)(2,1)} %bitcast.30), calls=%async_computation.2 | async-start | bytes 32768 | tf_op jit(solution)/shard_map/all_to_all | solution.py:31
  92.9 0.1 fusion
  93.0 6.5 %all-to-all-done.2 = bf16[8,1,8,128]{3,2,1,0:T(8,128)(2,1)S(1)} async-done(((bf16[8,1,8,128]{3,2,1,0:T(8,128)(2,1)}), bf16[8,1,8,128]{3,2,1,0:T(8,128)(2,1)S(1)}, u32[]{:S(2)}, u32[]{:S(2)}) %all-to-all-start.2) | async-done | bytes 16416 | tf_op jit(solution)/shard_map/all_to_all | solution.py:31
  99.4 0.6 gather_fusion.8
  100.0 0.2 convolution_bitcast_fusion.4
  100.2 0.1 fusion.10
  100.3 0.1 fusion.13
  100.5 0.1 fusion.15
  100.6 39.3 %all-reduce = (f32[32,8]{0,1:T(8,128)S(1)}, f32[8,8]{0,1:T(8,128)S(1)}, f32[32,32]{1,0:T(8,128)S(1)}) all-reduce(f32[32,8]{0,1:T(8,128)S(1)} %fusion.15, f32[8,8]{0,1:T(8,128)S(1)} %fusion.13, f32[32,32]{1,0:T(8,128)S(1)} %fusion), channel_id=1, replica_groups=mesh['group'=4,'member'=8] {'group','member'}, use_global_device_ids=true, to_apply=%region_1.0 | all-reduce | flops 1344 | bytes 10752 | tf_op jit(solution)/shard_map/psum | solution.py:115
  139.8 0.1 fusion.1
  140.0 0.1 fusion.36
  140.1 0.1 fusion.12
  140.2 0.2 copy-done.7
  140.4 0.2 convolution_add_fusion.5
  140.6 0.1 copy.30
  140.7 0.6 copy-done.8
  141.3 0.7 cholesky.17
  142.0 0.6 compare_reduce_fusion
  142.7 0.6 fusion.20
  143.4 0.6 custom-call.6
  144.0 0.2 convolution_bitcast_fusion.8
  144.2 0.8 convolution_bitcast_fusion.1
  (28 shorter events, 0.2 us)
Async XLA Ops:
  0.6 64.3 %copy-start = (bf16[1024,256]{1,0:T(8,128)(2,1)S(1)}, bf16[1024,256]{1,0:T(8,128)(2,1)}, u32[]{:S(2)}) copy-start(bf16[1024,256]{1,0:T(8,128)(2,1)} %param.18) | copy-start | bytes 1572868
  2.9 3.7 %copy-start.10 = (s32[1,8,1]{1,2,0:T(1,128)S(1)}, s32[1,8,1]{1,2,0:T(1,128)}, u32[]{:S(2)}) copy-start(s32[1,8,1]{1,2,0:T(1,128)} %param.12) | copy-start | bytes 100
  2.9 11.8 %collective-permute-start = (bf16[1,4,8,128]{3,2,1,0:T(8,128)(2,1)S(1)}, bf16[1,4,8,128]{3,2,1,0:T(8,128)(2,1)S(1)}, u32[]{:S(2)}, u32[]{:S(2)}) collective-permute-start(bf16[1,4,8,128]{3,2,1,0:T(8,128)(2,1)S(1)} %bitcast.145), channel_id=1, source_target_pairs={{0,8},{8,16},{16,24},{1,9},{9,17},{17,25},{2,10},{10,18},{18,26},{... | collective-permute-start | bytes 24584 | tf_op jit(solution)/shard_map/ppermute | solution.py:20
  5.3 9.4 %collective-permute-start.1 = (bf16[1,4,8,128]{3,2,1,0:T(8,128)(2,1)S(1)}, bf16[1,4,8,128]{3,2,1,0:T(8,128)(2,1)S(1)}, u32[]{:S(2)}, u32[]{:S(2)}) collective-permute-start(bf16[1,4,8,128]{3,2,1,0:T(8,128)(2,1)S(1)} %bitcast.146), channel_id=1, source_target_pairs={{8,0},{16,8},{24,16},{9,1},{17,9},{25,17},{10,2},{18,10},{26,18},{... | collective-permute-start | bytes 24584 | tf_op jit(solution)/shard_map/ppermute | solution.py:22
  7.8 6.8 %copy-start.9 = (s32[2,8]{1,0:T(2,128)S(1)}, s32[2,8]{1,0:T(2,128)}, u32[]{:S(2)}) copy-start(s32[2,8]{1,0:T(2,128)} %param.11) | copy-start | bytes 196
  7.8 13.3 %all-to-all-start = ((bf16[8,1,8,128]{3,2,1,0:T(8,128)(2,1)}), bf16[8,1,8,128]{3,2,1,0:T(8,128)(2,1)S(1)}, u32[]{:S(2)}, u32[]{:S(2)}) async-start(bf16[8,1,8,128]{3,2,1,0:T(8,128)(2,1)} %bitcast.5), calls=%async_computation | async-start | bytes 32768 | tf_op jit(solution)/shard_map/all_to_all | solution.py:31
  21.8 1.3 copy-start.2
  21.8 1.3 copy-start.3
  21.8 1.3 copy-start.6
  23.1 0.7 copy-start.11
  23.3 55.1 %copy-start.1 = (bf16[2,8,128,128]{3,2,1,0:T(8,128)(2,1)S(1)}, bf16[2,8,128,128]{3,2,1,0:T(8,128)(2,1)}, u32[]{:S(2)}) copy-start(bf16[2,8,128,128]{3,2,1,0:T(8,128)(2,1)} %param.10) | copy-start | bytes 1572868
  66.6 11.2 %all-to-all-start.1 = ((bf16[8,1,8,128]{3,2,1,0:T(8,128)(2,1)}), bf16[8,1,8,128]{3,2,1,0:T(8,128)(2,1)S(1)}, u32[]{:S(2)}, u32[]{:S(2)}) async-start(bf16[8,1,8,128]{3,2,1,0:T(8,128)(2,1)} %bitcast.21), calls=%async_computation.1 | async-start | bytes 32768 | tf_op jit(solution)/shard_map/all_to_all | solution.py:31
  71.6 2.6 %collective-permute-start.2 = (bf16[1,4,8,128]{3,2,1,0:T(8,128)(2,1)S(1)}, bf16[1,4,8,128]{3,2,1,0:T(8,128)(2,1)S(1)}, u32[]{:S(2)}, u32[]{:S(2)}) collective-permute-start(bf16[1,4,8,128]{3,2,1,0:T(8,128)(2,1)S(1)} %bitcast.149), channel_id=1, source_target_pairs={{0,8},{8,16},{16,24},{1,9},{9,17},{17,25},{2,10},{10,18},{18,26},{... | collective-permute-start | bytes 24584 | tf_op jit(solution)/shard_map/ppermute | solution.py:20
  72.9 4.9 %collective-permute-start.3 = (bf16[1,4,8,128]{3,2,1,0:T(8,128)(2,1)S(1)}, bf16[1,4,8,128]{3,2,1,0:T(8,128)(2,1)S(1)}, u32[]{:S(2)}, u32[]{:S(2)}) collective-permute-start(bf16[1,4,8,128]{3,2,1,0:T(8,128)(2,1)S(1)} %bitcast.150), channel_id=1, source_target_pairs={{8,0},{16,8},{24,16},{9,1},{17,9},{25,17},{10,2},{18,10},{26,18},{... | collective-permute-start | bytes 24584 | tf_op jit(solution)/shard_map/ppermute | solution.py:22
  78.4 0.8 copy-start.5
  79.5 20.7 %copy-start.4 = (bf16[2,8,128]{2,1,0:T(8,128)(2,1)}, bf16[2,8,128]{2,1,0:T(8,128)(2,1)S(1)}, u32[]{:S(2)}) copy-start(bf16[2,8,128]{2,1,0:T(8,128)(2,1)S(1)} %fusion.9) | copy-start | bytes 12292
  81.2 11.7 %collective-permute-start.4 = (bf16[1,4,8,128]{3,2,1,0:T(8,128)(2,1)S(1)}, bf16[1,4,8,128]{3,2,1,0:T(8,128)(2,1)S(1)}, u32[]{:S(2)}, u32[]{:S(2)}) collective-permute-start(bf16[1,4,8,128]{3,2,1,0:T(8,128)(2,1)S(1)} %bitcast.147), channel_id=1, source_target_pairs={{0,8},{8,16},{16,24},{1,9},{9,17},{17,25},{2,10},{10,18},{18,26},{... | collective-permute-start | bytes 24584 | tf_op jit(solution)/shard_map/ppermute | solution.py:20
  85.5 7.4 %collective-permute-start.5 = (bf16[1,4,8,128]{3,2,1,0:T(8,128)(2,1)S(1)}, bf16[1,4,8,128]{3,2,1,0:T(8,128)(2,1)S(1)}, u32[]{:S(2)}, u32[]{:S(2)}) collective-permute-start(bf16[1,4,8,128]{3,2,1,0:T(8,128)(2,1)S(1)} %bitcast.148), channel_id=1, source_target_pairs={{8,0},{16,8},{24,16},{9,1},{17,9},{25,17},{10,2},{18,10},{26,18},{... | collective-permute-start | bytes 24584 | tf_op jit(solution)/shard_map/ppermute | solution.py:22
  86.8 12.6 %all-to-all-start.2 = ((bf16[8,1,8,128]{3,2,1,0:T(8,128)(2,1)}), bf16[8,1,8,128]{3,2,1,0:T(8,128)(2,1)S(1)}, u32[]{:S(2)}, u32[]{:S(2)}) async-start(bf16[8,1,8,128]{3,2,1,0:T(8,128)(2,1)} %bitcast.30), calls=%async_computation.2 | async-start | bytes 32768 | tf_op jit(solution)/shard_map/all_to_all | solution.py:31
  139.8 0.6 copy-start.7
  140.7 0.6 copy-start.8
where the time goes:
time: 146 us; the launch traced here: 145 us
  blocking collectives  80.3 us (55%)
  starting transfers between devices  29.1 us (20%)
  waiting for transfers between devices  16.5 us (11%)
  local copies, waits for them, and re-layouts  8.97 us (6%)
  matrix products  5.74 us (4%)
  other arithmetic  3.44 us (2%)
    psum x1, blocking collectives, local(): lax.psum(spread, ('group', 'member')).reshape(groups * CTG, NVEC, TILE)  41 us
    psum x1, blocking collectives, local(): lax.psum((coeff_part, self_part, basis_part), ('group', 'member'))  39.3 us
    all_to_all x3, starting transfers between devices, extend_tiles(): lax.all_to_all(outgoing, 'member', split_axis=0, concat_axis=0, tiled=True)  17.3 us
    all_to_all x3, waiting for transfers between devices, extend_tiles(): lax.all_to_all(outgoing, 'member', split_axis=0, concat_axis=0, tiled=True)  12.9 us
    ppermute x3, starting transfers between devices, extended_2(): lax.ppermute(tail, axis, [(i, (i + 1) % count) for i in range(ends)])  7.99 us
    ppermute x3, starting transfers between devices, extended_2(): lax.ppermute(head, axis, [((i + 1) % count, i) for i in range(ends)])  3.88 us
    ppermute x3, waiting for transfers between devices, extended_2(): lax.ppermute(head, axis, [((i + 1) % count, i) for i in range(ends)])  3.57 us
    gather x3, local copies, waits for them, and re-layouts, extend_tiles(): values[member_send[0].reshape(-1)].reshape(members, GH, NVEC, TILE)  3.5 us
  transfers between devices with their start and end apart: 9, of which 3 were waited for; matrix products, arithmetic and copies ran while one was open for 1% of the time, Pallas kernels for 0%

commit v1 on v0

--- a/solution.py
+++ b/solution.py
@@ -113,7 +113,7 @@
         * scale_rows
     )
     coefficients, self_total, basis_total = lax.psum(
-        (coeff_part, self_part, basis_part), ("group", "member")
+        lax.psum((coeff_part, self_part, basis_part), "group"), "member"
     )
     remainder = applied.astype(jnp.float32) - exact_product("pc,tpi->tci", coefficients, basis_wide)
     cross = exact_product("pc,pd->cd", coefficients, coefficients)

time: 146 us -> 150 us (1.027)
  blocking collectives: 80.3 us -> 84.8 us
    psum x1 -> x2, blocking collectives: 39.3 us -> 43.8 us  [the longest x1 33.5 us: local(): lax.psum(lax.psum((coeff_part, self_part, basis_part), 'group'), 'member')]
where the time goes in v1:
time: 150 us; the launch traced here: 149 us
  blocking collectives  84.8 us (57%)
  starting transfers between devices  29.1 us (19%)
  waiting for transfers between devices  16.5 us (11%)
  local copies, waits for them, and re-layouts  8.96 us (6%)
  matrix products  5.74 us (4%)
  other arithmetic  3.44 us (2%)
    psum x1, blocking collectives, local(): lax.psum(spread, ('group', 'member')).reshape(groups * CTG, NVEC, TILE)  41 us
    psum x1, blocking collectives, local(): lax.psum(lax.psum((coeff_part, self_part, basis_part), 'group'), 'member')  33.5 us
    all_to_all x3, starting transfers between devices, extend_tiles(): lax.all_to_all(outgoing, 'member', split_axis=0, concat_axis=0, tiled=True)  17.3 us
    all_to_all x3, waiting for transfers between devices, extend_tiles(): lax.all_to_all(outgoing, 'member', split_axis=0, concat_axis=0, tiled=True)  12.9 us
    psum x1, blocking collectives, local(): lax.psum((coeff_part, self_part, basis_part), 'group')  10.3 us
    ppermute x3, starting transfers between devices, extended_2(): lax.ppermute(tail, axis, [(i, (i + 1) % count) for i in range(ends)])  7.99 us
    ppermute x3, starting transfers between devices, extended_2(): lax.ppermute(head, axis, [((i + 1) % count, i) for i in range(ends)])  3.88 us
    ppermute x3, waiting for transfers between devices, extended_2(): lax.ppermute(head, axis, [((i + 1) % count, i) for i in range(ends)])  3.57 us
  transfers between devices with their start and end apart: 9, of which 3 were waited for; matrix products, arithmetic and copies ran while one was open for 1% of the time, Pallas kernels for 0%

profile of v1, /device:TPU:0, one launch (start us, length us, event | category | flops | bytes accessed | tf_op | source)
XLA Modules:
  0.0 149.4 jit_solution(5475354075779284654)
XLA Ops:
  0.6 0.0 copy-start
  0.6 0.7 fusion.33
  1.4 1.0 convolution_convert_fusion
  2.4 0.6 gather_fusion.1
  2.9 0.0 copy-start.10
  2.9 2.4 %collective-permute-start = (bf16[1,4,8,128]{3,2,1,0:T(8,128)(2,1)S(1)}, bf16[1,4,8,128]{3,2,1,0:T(8,128)(2,1)S(1)}, u32[]{:S(2)}, u32[]{:S(2)}) collective-permute-start(bf16[1,4,8,128]{3,2,1,0:T(8,128)(2,1)S(1)} %bitcast.145), channel_id=1, source_target_pairs={{0,8},{8,16},{16,24},{1,9},{9,17},{17,25},{2,10},{10,18},{18,26},{... | collective-permute-start | bytes 24584 | tf_op jit(solution)/shard_map/ppermute | solution.py:20
  5.3 1.3 collective-permute-start.1
  6.7 1.2 gather_fusion
  7.8 6.8 %all-to-all-start = ((bf16[8,1,8,128]{3,2,1,0:T(8,128)(2,1)}), bf16[8,1,8,128]{3,2,1,0:T(8,128)(2,1)S(1)}, u32[]{:S(2)}, u32[]{:S(2)}) async-start(bf16[8,1,8,128]{3,2,1,0:T(8,128)(2,1)} %bitcast.5), calls=%async_computation | async-start | bytes 32768 | tf_op jit(solution)/shard_map/all_to_all | solution.py:31
  14.6 0.1 reshape.126
  14.7 0.0 collective-permute-done
  14.7 0.0 collective-permute-done.1
  14.7 6.5 %all-to-all-done = bf16[8,1,8,128]{3,2,1,0:T(8,128)(2,1)S(1)} async-done(((bf16[8,1,8,128]{3,2,1,0:T(8,128)(2,1)}), bf16[8,1,8,128]{3,2,1,0:T(8,128)(2,1)S(1)}, u32[]{:S(2)}, u32[]{:S(2)}) %all-to-all-start) | async-done | bytes 16416 | tf_op jit(solution)/shard_map/all_to_all | solution.py:31
  21.2 0.6 gather_fusion.2
  21.8 0.0 copy-start.3
  21.8 0.0 copy-start.6
  21.8 1.3 convolution_bitcast_fusion.7
  23.1 0.0 copy-start.11
  23.1 0.2 fusion.11
  23.3 0.4 copy-done.11
  23.7 0.1 fusion.3
  23.9 41.0 %psum.49 = bf16[4,2,8,128]{3,1,2,0:T(2,128)(2,1)S(1)} all-reduce(f32[4,2,8,128]{3,1,2,0:T(2,128)S(1)} %fusion.3), channel_id=1, replica_groups=mesh['group'=4,'member'=8] {'group','member'}, use_global_device_ids=true, to_apply=%region_0.0 | all-reduce | flops 8192 | bytes 49152 | tf_op jit(solution)/shard_map/psum | solution.py:85
  64.9 0.2 fusion.16
  65.1 0.2 fusion.24
  65.3 0.1 fusion.7
  65.4 1.2 gather_fusion.3
  66.6 4.5 %all-to-all-start.1 = ((bf16[8,1,8,128]{3,2,1,0:T(8,128)(2,1)}), bf16[8,1,8,128]{3,2,1,0:T(8,128)(2,1)S(1)}, u32[]{:S(2)}, u32[]{:S(2)}) async-start(bf16[8,1,8,128]{3,2,1,0:T(8,128)(2,1)} %bitcast.21), calls=%async_computation.1 | async-start | bytes 32768 | tf_op jit(solution)/shard_map/all_to_all | solution.py:31
  71.1 0.6 gather_fusion.4
  71.6 1.3 collective-permute-start.2
  72.9 1.3 collective-permute-start.3
  74.3 3.6 %collective-permute-done.3 = bf16[1,4,8,128]{3,2,1,0:T(8,128)(2,1)S(1)} collective-permute-done((bf16[1,4,8,128]{3,2,1,0:T(8,128)(2,1)S(1)}, bf16[1,4,8,128]{3,2,1,0:T(8,128)(2,1)S(1)}, u32[]{:S(2)}, u32[]{:S(2)}) %collective-permute-start.3) | collective-permute-done | bytes 8224 | tf_op jit(solution)/shard_map/ppermute | solution.py:22
  77.8 0.0 all-to-all-done.1
  77.8 0.6 gather_fusion.5
  78.4 0.0 copy-start.5
  78.4 0.2 convolution_bitcast_fusion.5
  78.6 0.6 copy-done.5
  79.3 0.2 fusion.9
  79.5 1.2 gather_fusion.6
  80.7 0.6 gather_fusion.7
  81.2 4.3 %collective-permute-start.4 = (bf16[1,4,8,128]{3,2,1,0:T(8,128)(2,1)S(1)}, bf16[1,4,8,128]{3,2,1,0:T(8,128)(2,1)S(1)}, u32[]{:S(2)}, u32[]{:S(2)}) collective-permute-start(bf16[1,4,8,128]{3,2,1,0:T(8,128)(2,1)S(1)} %bitcast.147), channel_id=1, source_target_pairs={{0,8},{8,16},{16,24},{1,9},{9,17},{17,25},{2,10},{10,18},{18,26},{... | collective-permute-start | bytes 24584 | tf_op jit(solution)/shard_map/ppermute | solution.py:20
  85.5 1.3 collective-permute-start.5
  86.8 6.0 %all-to-all-start.2 = ((bf16[8,1,8,128]{3,2,1,0:T(8,128)(2,1)}), bf16[8,1,8,128]{3,2,1,0:T(8,128)(2,1)S(1)}, u32[]{:S(2)}, u32[]{:S(2)}) async-start(bf16[8,1,8,128]{3,2,1,0:T(8,128)(2,1)} %bitcast.30), calls=%async_computation.2 | async-start | bytes 32768 | tf_op jit(solution)/shard_map/all_to_all | solution.py:31
  92.8 0.1 fusion
  93.0 6.5 %all-to-all-done.2 = bf16[8,1,8,128]{3,2,1,0:T(8,128)(2,1)S(1)} async-done(((bf16[8,1,8,128]{3,2,1,0:T(8,128)(2,1)}), bf16[8,1,8,128]{3,2,1,0:T(8,128)(2,1)S(1)}, u32[]{:S(2)}, u32[]{:S(2)}) %all-to-all-start.2) | async-done | bytes 16416 | tf_op jit(solution)/shard_map/all_to_all | solution.py:31
  99.4 0.6 gather_fusion.8
  100.0 0.2 convolution_bitcast_fusion.4
  100.2 0.1 fusion.10
  100.3 0.1 fusion.13
  100.5 0.1 fusion.15
  100.6 10.3 %all-reduce.1 = (f32[32,8]{0,1:T(8,128)S(1)}, f32[8,8]{0,1:T(8,128)S(1)}, f32[32,32]{1,0:T(8,128)S(1)}) all-reduce(f32[32,8]{0,1:T(8,128)S(1)} %fusion.15, f32[8,8]{0,1:T(8,128)S(1)} %fusion.13, f32[32,32]{1,0:T(8,128)S(1)} %fusion), channel_id=1, replica_groups=mesh['group'=4,'member'=8] {'group'}, use_global_device_ids=true, to_apply=%region_1.0 | all-reduce | flops 1344 | bytes 10752 | tf_op jit(solution)/shard_map/psum | solution.py:116
  110.9 33.5 %all-reduce = (f32[32,8]{0,1:T(8,128)S(1)}, f32[8,8]{0,1:T(8,128)S(1)}, f32[32,32]{1,0:T(8,128)S(1)}) all-reduce(f32[32,8]{0,1:T(8,128)S(1)} %get-tuple-element.15, f32[8,8]{0,1:T(8,128)S(1)} %get-tuple-element.16, f32[32,32]{1,0:T(8,128)S(1)} %get-tuple-element.17), channel_id=1, replica_groups=mesh['group'=4,'member'=8] {'member'}, use_global_device_ids=true, to_apply=%region_2.0 | all-reduce | flops 1344 | bytes 10752 | tf_op jit(solution)/shard_map/psum | solution.py:115
  144.3 0.1 fusion.1
  144.5 0.1 fusion.36
  144.6 0.1 fusion.12
  144.7 0.2 copy-done.7
  144.9 0.2 convolution_add_fusion.5
  145.1 0.1 copy.30
  145.2 0.6 copy-done.8
  145.8 0.7 cholesky.17
  146.6 0.6 compare_reduce_fusion
  147.2 0.6 fusion.20
  147.9 0.6 custom-call.6
  148.5 0.2 convolution_bitcast_fusion.8
  148.7 0.8 convolution_bitcast_fusion.1
  (29 shorter events, 0.2 us)
Async XLA Ops:
  0.6 64.3 %copy-start = (bf16[1024,256]{1,0:T(8,128)(2,1)S(1)}, bf16[1024,256]{1,0:T(8,128)(2,1)}, u32[]{:S(2)}) copy-start(bf16[1024,256]{1,0:T(8,128)(2,1)} %param.18) | copy-start | bytes 1572868
  2.9 3.7 %copy-start.10 = (s32[1,8,1]{1,2,0:T(1,128)S(1)}, s32[1,8,1]{1,2,0:T(1,128)}, u32[]{:S(2)}) copy-start(s32[1,8,1]{1,2,0:T(1,128)} %param.12) | copy-start | bytes 100
  2.9 11.8 %collective-permute-start = (bf16[1,4,8,128]{3,2,1,0:T(8,128)(2,1)S(1)}, bf16[1,4,8,128]{3,2,1,0:T(8,128)(2,1)S(1)}, u32[]{:S(2)}, u32[]{:S(2)}) collective-permute-start(bf16[1,4,8,128]{3,2,1,0:T(8,128)(2,1)S(1)} %bitcast.145), channel_id=1, source_target_pairs={{0,8},{8,16},{16,24},{1,9},{9,17},{17,25},{2,10},{10,18},{18,26},{... | collective-permute-start | bytes 24584 | tf_op jit(solution)/shard_map/ppermute | solution.py:20
  5.3 9.4 %collective-permute-start.1 = (bf16[1,4,8,128]{3,2,1,0:T(8,128)(2,1)S(1)}, bf16[1,4,8,128]{3,2,1,0:T(8,128)(2,1)S(1)}, u32[]{:S(2)}, u32[]{:S(2)}) collective-permute-start(bf16[1,4,8,128]{3,2,1,0:T(8,128)(2,1)S(1)} %bitcast.146), channel_id=1, source_target_pairs={{8,0},{16,8},{24,16},{9,1},{17,9},{25,17},{10,2},{18,10},{26,18},{... | collective-permute-start | bytes 24584 | tf_op jit(solution)/shard_map/ppermute | solution.py:22
  7.8 6.8 %copy-start.9 = (s32[2,8]{1,0:T(2,128)S(1)}, s32[2,8]{1,0:T(2,128)}, u32[]{:S(2)}) copy-start(s32[2,8]{1,0:T(2,128)} %param.11) | copy-start | bytes 196
  7.8 13.3 %all-to-all-start = ((bf16[8,1,8,128]{3,2,1,0:T(8,128)(2,1)}), bf16[8,1,8,128]{3,2,1,0:T(8,128)(2,1)S(1)}, u32[]{:S(2)}, u32[]{:S(2)}) async-start(bf16[8,1,8,128]{3,2,1,0:T(8,128)(2,1)} %bitcast.5), calls=%async_computation | async-start | bytes 32768 | tf_op jit(solution)/shard_map/all_to_all | solution.py:31
  21.7 1.3 copy-start.2
  21.8 1.3 copy-start.3
  21.8 1.3 copy-start.6
  23.1 0.7 copy-start.11
  23.3 55.1 %copy-start.1 = (bf16[2,8,128,128]{3,2,1,0:T(8,128)(2,1)S(1)}, bf16[2,8,128,128]{3,2,1,0:T(8,128)(2,1)}, u32[]{:S(2)}) copy-start(bf16[2,8,128,128]{3,2,1,0:T(8,128)(2,1)} %param.10) | copy-start | bytes 1572868
  66.6 11.2 %all-to-all-start.1 = ((bf16[8,1,8,128]{3,2,1,0:T(8,128)(2,1)}), bf16[8,1,8,128]{3,2,1,0:T(8,128)(2,1)S(1)}, u32[]{:S(2)}, u32[]{:S(2)}) async-start(bf16[8,1,8,128]{3,2,1,0:T(8,128)(2,1)} %bitcast.21), calls=%async_computation.1 | async-start | bytes 32768 | tf_op jit(solution)/shard_map/all_to_all | solution.py:31
  71.6 2.6 %collective-permute-start.2 = (bf16[1,4,8,128]{3,2,1,0:T(8,128)(2,1)S(1)}, bf16[1,4,8,128]{3,2,1,0:T(8,128)(2,1)S(1)}, u32[]{:S(2)}, u32[]{:S(2)}) collective-permute-start(bf16[1,4,8,128]{3,2,1,0:T(8,128)(2,1)S(1)} %bitcast.149), channel_id=1, source_target_pairs={{0,8},{8,16},{16,24},{1,9},{9,17},{17,25},{2,10},{10,18},{18,26},{... | collective-permute-start | bytes 24584 | tf_op jit(solution)/shard_map/ppermute | solution.py:20
  72.9 4.9 %collective-permute-start.3 = (bf16[1,4,8,128]{3,2,1,0:T(8,128)(2,1)S(1)}, bf16[1,4,8,128]{3,2,1,0:T(8,128)(2,1)S(1)}, u32[]{:S(2)}, u32[]{:S(2)}) collective-permute-start(bf16[1,4,8,128]{3,2,1,0:T(8,128)(2,1)S(1)} %bitcast.150), channel_id=1, source_target_pairs={{8,0},{16,8},{24,16},{9,1},{17,9},{25,17},{10,2},{18,10},{26,18},{... | collective-permute-start | bytes 24584 | tf_op jit(solution)/shard_map/ppermute | solution.py:22
  78.4 0.8 copy-start.5
  79.5 20.7 %copy-start.4 = (bf16[2,8,128]{2,1,0:T(8,128)(2,1)}, bf16[2,8,128]{2,1,0:T(8,128)(2,1)S(1)}, u32[]{:S(2)}) copy-start(bf16[2,8,128]{2,1,0:T(8,128)(2,1)S(1)} %fusion.9) | copy-start | bytes 12292
  81.2 11.7 %collective-permute-start.4 = (bf16[1,4,8,128]{3,2,1,0:T(8,128)(2,1)S(1)}, bf16[1,4,8,128]{3,2,1,0:T(8,128)(2,1)S(1)}, u32[]{:S(2)}, u32[]{:S(2)}) collective-permute-start(bf16[1,4,8,128]{3,2,1,0:T(8,128)(2,1)S(1)} %bitcast.147), channel_id=1, source_target_pairs={{0,8},{8,16},{16,24},{1,9},{9,17},{17,25},{2,10},{10,18},{18,26},{... | collective-permute-start | bytes 24584 | tf_op jit(solution)/shard_map/ppermute | solution.py:20
  85.5 7.4 %collective-permute-start.5 = (bf16[1,4,8,128]{3,2,1,0:T(8,128)(2,1)S(1)}, bf16[1,4,8,128]{3,2,1,0:T(8,128)(2,1)S(1)}, u32[]{:S(2)}, u32[]{:S(2)}) collective-permute-start(bf16[1,4,8,128]{3,2,1,0:T(8,128)(2,1)S(1)} %bitcast.148), channel_id=1, source_target_pairs={{8,0},{16,8},{24,16},{9,1},{17,9},{25,17},{10,2},{18,10},{26,18},{... | collective-permute-start | bytes 24584 | tf_op jit(solution)/shard_map/ppermute | solution.py:22
  86.8 12.6 %all-to-all-start.2 = ((bf16[8,1,8,128]{3,2,1,0:T(8,128)(2,1)}), bf16[8,1,8,128]{3,2,1,0:T(8,128)(2,1)S(1)}, u32[]{:S(2)}, u32[]{:S(2)}) async-start(bf16[8,1,8,128]{3,2,1,0:T(8,128)(2,1)} %bitcast.30), calls=%async_computation.2 | async-start | bytes 32768 | tf_op jit(solution)/shard_map/all_to_all | solution.py:31
  144.3 0.6 copy-start.7
  145.2 0.6 copy-start.8
